TPU v7x, 128 devices: a whole 4x4x4 slice. The times are simulated.
128 devices in a mesh: section: 4 (over y), dp: 32 (over x, z, core).
Axes of the slice: x: 4, y: 4, z: 4, core: 2. Of those that a mesh axis runs over, the one named last changes fastest.
Arguments:
- inputs: bfloat16 [4096, 1600], P('dp'), may hold values from -6 to 6
- targets: bfloat16 [4096, 1600], P('dp'), may hold values from -6 to 6
- weight_in: bfloat16 [4, 1600, 3200], P('section'), may hold values from -0.15625 to 0.15625
- hidden_bias: float32 [4, 3200], P('section'), may hold values from -3 to 3
- norm_gain: float32 [4, 1600], P('section'), may hold values from 0.5 to 1.5
- weight_out: bfloat16 [4, 3200, 1600], P('section'), may hold values from -0.109375 to 0.109375
- current: float32 [4, 3200, 1600], P('section', 'dp')
- previous: float32 [4, 3200, 1600], P('section', 'dp')
- older_basis: float32 [2, 4, 3200, 1600], P(None, 'section', 'dp')
- beta_before: float32 [1], replicated, may hold values from 1 to 4
Outputs:
- next_vector: float32 [4, 3200, 1600], P('section', 'dp')
- tridiagonal_entries: float32 [2], replicated
All inputs are finite; a program needn't handle non-finite values.
Results may differ from a plain program's by a relative error of at most 0.012.
Values may be sent and summed in bfloat16 or wider, within the bound.
A program may use at most 192 MiB of HBM per device.

v0:
```python
from functools import partial
import functools

import jax
import jax.numpy as jnp
from jax import lax
from jax.sharding import Mesh
from jax.sharding import PartitionSpec as P

DP = ("dp_0", "dp_1", "dp_2")
SECTION_DP = ("section", "dp_0", "dp_1", "dp_2")


def laid_out(blocks, dim):
    dims = list(blocks.shape[1:])
    dims[dim] *= blocks.shape[0]
    return jnp.moveaxis(blocks, 0, dim).reshape(dims)


def gather_in_order(value, axes, turns):
    blocks = value[None]
    for k in turns:
        blocks = lax.all_gather(blocks, axes[k], axis=0, tiled=True)
    carried = [lax.axis_size(axes[k]) for k in reversed(turns)]
    blocks = blocks.reshape(*carried, *value.shape)
    turned = sorted(range(len(turns)), key=lambda place: turns[len(turns) - 1 - place])
    return blocks.transpose(*turned, *range(len(turns), blocks.ndim)).reshape(-1, *value.shape)


def gathered_by_axis(value, axes, turns, dim):
    return laid_out(gather_in_order(value, axes, turns), dim)


def from_behind(value, axis, steps):
    count = lax.axis_size(axis)
    initial, last = (max(0, -steps), min(count, count - steps))
    return lax.ppermute(value, axis, [(source, source + steps) for source in range(initial, last)])


def sent_together(arrays, axis, dim, along):
    ends, at = ([], 0)
    for a in arrays[:-1]:
        at += a.shape[along]
        ends.append(at)
    both = jnp.concatenate(arrays, axis=along)
    return tuple(jnp.split(lax.all_gather(both, axis, axis=dim, tiled=True), ends, axis=along))


def over_axes(value, axes):
    return functools.reduce(lax.psum, axes, value)


def gelu_tanh(values):
    return jax.nn.gelu(values, approximate=True)


def gelu_slope(values):
    return jax.jvp(gelu_tanh, (values,), (jnp.ones_like(values),))[1]


def gelu_bend(values):
    return jax.jvp(gelu_slope, (values,), (jnp.ones_like(values),))[1]


def normalize(values, gain_row):
    mean_value = jnp.mean(values, axis=-1, keepdims=True)
    centered = values - mean_value
    variance = jnp.mean(centered * centered, axis=-1, keepdims=True)
    return centered * lax.rsqrt(variance + 1e-05) * gain_row


def times_transposed(left, right):
    return lax.dot_general(
        left, right, (((1,), (1,)), ((), ())), preferred_element_type=jnp.float32
    )


def pick_block(stack, position):
    return lax.dynamic_index_in_dim(stack, position, 0, keepdims=False)


def store_block(stack, block, position, active):
    return jnp.where(active, lax.dynamic_update_index_in_dim(stack, block, position, 0), stack)


def body(
    inputs,
    targets,
    weight_in,
    hidden_bias,
    norm_gain,
    weight_out,
    current,
    previous,
    older_basis,
    beta_before,
):
    section_index = lax.axis_index("section")
    sections = lax.axis_size("section")
    replicas = lax.axis_size(DP)
    layer_in = weight_in[0]
    bias_row = hidden_bias[0]
    gain_row = norm_gain[0]
    layer_out = weight_out[0]
    direction = gathered_by_axis(
        current[0].astype(jnp.bfloat16), (("dp_0", "dp_1"), "dp_2"), (0, 1), 0
    )
    pieces = 2
    local_rows, width = inputs.shape
    hidden_width = layer_in.shape[1]
    block_rows = local_rows // pieces
    row_count = float(local_rows * replicas)
    blocks_in = inputs.reshape(pieces, block_rows, width)
    blocks_goal = targets.reshape(pieces, block_rows, width)
    empty_rows = jnp.zeros((block_rows, width), jnp.bfloat16)
    empty_hidden = jnp.zeros((block_rows, hidden_width), jnp.bfloat16)
    empty_pre = jnp.zeros((block_rows, hidden_width), jnp.float32)
    empty_stack = jnp.zeros((pieces, block_rows, width), jnp.bfloat16)
    hidden_stack = jnp.zeros((pieces, block_rows, hidden_width), jnp.bfloat16)
    pre_stack = jnp.zeros((pieces, block_rows, hidden_width), jnp.float32)
    kept_rows, kept_tangent = (empty_stack, empty_stack)
    final_rows, final_tangent = (empty_stack, empty_stack)
    hidden_dot_stack = hidden_stack
    preact_stack, preact_dot_stack = (pre_stack, pre_stack)
    arrived_rows, arrived_tangent = (empty_rows, empty_rows)
    tick_count = pieces + sections - 1

    def run_layer(operands):
        rows_float = operands[0].astype(jnp.float32)
        tangent_float = operands[1].astype(jnp.float32)
        normed, normed_dot = jax.jvp(
            partial(normalize, gain_row=gain_row), (rows_float,), (tangent_float,)
        )
        stacked_norm = jnp.concatenate(
            [normed.astype(jnp.bfloat16), normed_dot.astype(jnp.bfloat16)], axis=0
        )
        pre_both = jnp.dot(stacked_norm, layer_in, preferred_element_type=jnp.float32)
        preact = pre_both[:block_rows] + bias_row
        preact_dot = pre_both[block_rows:]
        hidden = gelu_tanh(preact).astype(jnp.bfloat16)
        hidden_dot = (gelu_slope(preact) * preact_dot).astype(jnp.bfloat16)
        out_both = jnp.dot(
            jnp.concatenate([hidden, hidden_dot], axis=0),
            layer_out,
            preferred_element_type=jnp.float32,
        )
        rows_out = rows_float + out_both[:block_rows]
        tangent_out = tangent_float + out_both[block_rows:]
        tangent_out = tangent_out + jnp.dot(hidden, direction, preferred_element_type=jnp.float32)
        return (
            rows_out.astype(jnp.bfloat16),
            tangent_out.astype(jnp.bfloat16),
            preact,
            preact_dot,
            hidden,
            hidden_dot,
        )

    def skip_layer(operands):
        return (empty_rows, empty_rows, empty_pre, empty_pre, empty_hidden, empty_hidden)

    for step_number in range(tick_count):
        micro_slot = step_number - section_index
        active = jnp.logical_and(micro_slot >= 0, micro_slot < pieces)
        position = jnp.clip(micro_slot, 0, pieces - 1)
        feed_rows = jnp.where(section_index == 0, pick_block(blocks_in, position), arrived_rows)
        feed_tangent = jnp.where(section_index == 0, empty_rows, arrived_tangent)
        out_rows, out_tangent, preact, preact_dot, hidden, hidden_dot = lax.cond(
            active, run_layer, skip_layer, (feed_rows, feed_tangent)
        )
        kept_rows = store_block(kept_rows, feed_rows, position, active)
        kept_tangent = store_block(kept_tangent, feed_tangent, position, active)
        final_rows = store_block(final_rows, out_rows, position, active)
        final_tangent = store_block(final_tangent, out_tangent, position, active)
        preact_stack = store_block(preact_stack, preact, position, active)
        preact_dot_stack = store_block(preact_dot_stack, preact_dot, position, active)
        hidden_stack = store_block(hidden_stack, hidden, position, active)
        hidden_dot_stack = store_block(hidden_dot_stack, hidden_dot, position, active)
        if step_number + 1 < tick_count:
            arrived_rows, arrived_tangent = from_behind((out_rows, out_tangent), "section", 1)

    def run_back(operands):
        rows_float = operands[0].astype(jnp.float32)
        tangent_float = operands[1].astype(jnp.float32)
        preact, preact_dot, grad_out, grad_dot_out = (
            operands[2],
            operands[3],
            operands[4],
            operands[5],
        )
        back_both = times_transposed(jnp.concatenate([grad_out, grad_dot_out], axis=0), layer_out)
        back_hidden = back_both[:block_rows]
        back_hidden_dot = back_both[block_rows:] + times_transposed(grad_out, direction)
        slope = gelu_slope(preact)
        pre_grad = (slope * back_hidden).astype(jnp.bfloat16)
        pre_grad_dot = (
            gelu_bend(preact) * preact_dot * back_hidden + slope * back_hidden_dot
        ).astype(jnp.bfloat16)
        norm_both = times_transposed(jnp.concatenate([pre_grad, pre_grad_dot], axis=0), layer_in)
        norm_grad = norm_both[:block_rows]
        norm_grad_dot = norm_both[block_rows:]

        def pull_back(values, cotangent):
            return jax.vjp(partial(normalize, gain_row=gain_row), values)[1](cotangent)[0]

        grad_in, grad_in_dot = jax.jvp(
            pull_back, (rows_float, norm_grad), (tangent_float, norm_grad_dot)
        )
        grad_next = (grad_out.astype(jnp.float32) + grad_in).astype(jnp.bfloat16)
        grad_dot_next = (grad_dot_out.astype(jnp.float32) + grad_in_dot).astype(jnp.bfloat16)
        return (grad_next, grad_dot_next)

    def skip_back(operands):
        return (empty_rows, empty_rows)

    grad_stack, grad_dot_stack = (empty_stack, empty_stack)
    arrived_grad, arrived_grad_dot = (empty_rows, empty_rows)
    last_section = sections - 1
    for step_number in range(tick_count):
        micro_slot = step_number - (last_section - section_index)
        active = jnp.logical_and(micro_slot >= 0, micro_slot < pieces)
        position = jnp.clip(micro_slot, 0, pieces - 1)
        top_rows = pick_block(final_rows, position).astype(jnp.float32)
        top_tangent = pick_block(final_tangent, position).astype(jnp.float32)
        goal_rows = pick_block(blocks_goal, position).astype(jnp.float32)
        own_grad = ((top_rows - goal_rows) / row_count).astype(jnp.bfloat16)
        own_grad_dot = (top_tangent / row_count).astype(jnp.bfloat16)
        feed_grad = jnp.where(section_index == last_section, own_grad, arrived_grad)
        feed_grad_dot = jnp.where(section_index == last_section, own_grad_dot, arrived_grad_dot)
        operands = (
            pick_block(kept_rows, position),
            pick_block(kept_tangent, position),
            pick_block(preact_stack, position),
            pick_block(preact_dot_stack, position),
            feed_grad,
            feed_grad_dot,
        )
        grad_next, grad_dot_next = lax.cond(active, run_back, skip_back, operands)
        grad_stack = store_block(grad_stack, feed_grad, position, active)
        grad_dot_stack = store_block(grad_dot_stack, feed_grad_dot, position, active)
        if step_number + 1 < tick_count:
            arrived_grad, arrived_grad_dot = from_behind((grad_next, grad_dot_next), "section", -1)
    hidden_rows = hidden_stack.reshape(local_rows, hidden_width)
    hidden_dot_rows = hidden_dot_stack.reshape(local_rows, hidden_width)
    grad_rows = grad_stack.reshape(local_rows, width)
    grad_dot_rows = grad_dot_stack.reshape(local_rows, width)
    hidden_share, slope_share = (
        lax.all_to_all(hidden_rows.T, DP, split_axis=0, concat_axis=1, tiled=True),
        lax.all_to_all(hidden_dot_rows.T, DP, split_axis=0, concat_axis=1, tiled=True),
    )
    gathered = sent_together((grad_rows, grad_dot_rows), DP, 0, 1)
    running = jnp.dot(slope_share, gathered[0], preferred_element_type=jnp.float32)
    hvp = (running + jnp.dot(hidden_share, gathered[1], preferred_element_type=jnp.float32))[None]
    entry_count = float(hvp.size * sections * replicas)
    basis = jnp.concatenate([older_basis, previous[None], current[None]], axis=0)
    members = basis.shape[0]
    stacked = jnp.concatenate([basis, hvp[None]], axis=0).reshape(members + 1, -1)
    local_gram = lax.dot_general(
        stacked,
        stacked,
        (((1,), (1,)), ((), ())),
        precision=lax.Precision.HIGHEST,
        preferred_element_type=jnp.float32,
    )
    gram = over_axes(local_gram, SECTION_DP) / entry_count
    basis_gram = gram[:members, :members]
    cross = gram[:members, members]
    square_hvp = gram[members, members]
    indices = jnp.arange(members)
    weights_start = jnp.where(indices == members - 2, -beta_before[0], 0.0)
    alpha_value = cross[members - 1] + jnp.sum(weights_start * basis_gram[:, members - 1])
    weights_first = weights_start - jnp.where(indices == members - 1, alpha_value, 0.0)
    coeffs = cross + jnp.sum(basis_gram * weights_first[:, None], axis=0)
    weights_second = weights_first - coeffs
    quadratic = jnp.sum(weights_second[:, None] * basis_gram * weights_second[None, :])
    square_second = square_hvp + 2.0 * jnp.sum(weights_second * cross) + quadratic
    beta_value = jnp.sqrt(jnp.maximum(square_second, 0.0) + 1e-06)
    second = hvp + jnp.sum(weights_second[:, None, None, None] * basis, axis=0)
    return (second / beta_value, jnp.stack([alpha_value, beta_value]))


def solution(mesh):
    finer = Mesh(
        mesh.devices.reshape(mesh.shape["section"], 4, 4, 2), ("section", "dp_0", "dp_1", "dp_2")
    )
    in_specs = (
        P(DP, None),
        P(DP, None),
        P("section", None, None),
        P("section", None),
        P("section", None),
        P("section", None, None),
        P("section", DP, None),
        P("section", DP, None),
        P(None, "section", DP, None),
        P(),
    )
    out_specs = (P("section", DP, None), P())
    return jax.shard_map(body, mesh=finer, in_specs=in_specs, out_specs=out_specs, check_vma=False)
```

profile of v0, /device:TPU:8, one launch (start us, length us, event | category | flops | bytes accessed | tf_op | source)
XLA Modules:
  0.0 730.4 jit_solution(5869003339484082788)
XLA Ops:
  9.1 61.6 %all-gather.4.cloned.1.call-done = bf16[16,100,1600]{2,1,0:T(8,128)(2,1)} async-done(((bf16[1,100,1600]{2,1,0:T(8,128)(2,1)}), bf16[16,100,1600]{2,1,0:T(8,128)(2,1)}) %all-gather.4.cloned.1.call-update) | async-done | bytes 5120016 | tf_op jit(solution)/shard_map/all_gather | solution.py:23
  70.8 5.6 copy.180
  78.7 17.5 %copy.178 = bf16[1,3200,1600]{2,1,0:T(8,128)(2,1)} copy(bf16[1,3200,1600]{1,2,0:T(8,128)(2,1)} %param.33) | data formatting | bytes 20480000 | tf_op args[5]
  101.7 10.0 %copy.280 = bf16[2,16,100,1600]{3,2,0,1:T(8,128)(2,1)} copy(bf16[2,16,100,1600]{3,1,0,2:T(8,128)(2,1)} %bitcast.647) | data formatting | bytes 20480000 | tf_op jit(solution)/shard_map/reshape | solution.py:25
  111.7 14.7 %reshape_reshape.3 = bf16[3200,1600]{1,0:T(8,128)(2,1)} reshape(bf16[16,2,100,1600]{3,2,1,0:T(8,128)(2,1)} %bitcast.644) | data formatting | bytes 20480000 | tf_op jit(solution)/shard_map/reshape;reshape | solution.py:17
  126.5 11.8 %conditional.9 = (f32[64,3200]{1,0:T(8,128)}, f32[64,3200]{1,0:T(8,128)S(1)}, bf16[1,64,3200]{2,1,0:T(8,128)(2,1)S(1)}, bf16[1,64,3200]{2,1,0:T(8,128)(2,1)}, bf...) conditional(s32[]{:T(128)} %convert_element_type.470, () %tuple.151, (bf16[1,64,1600]{2,1,0:T(8,128)(2,1)S(1)}, ...), branch_computations={%region_0.1_spmd, %region_1.5_spmd} | conditional | flops 3289190656 | bytes 78807200 | solution.py:168
  145.5 14.4 %collective-permute-done = bf16[64,1600]{1,0:T(8,128)(2,1)S(1)} collective-permute-done((bf16[64,1600]{1,0:T(8,128)(2,1)S(1)}, bf16[64,1600]{1,0:T(8,128)(2,1)S(1)}, u32[]{:S(2)}, u32[]{:S(2)}) %collective-permute-start) | collective-permute-done | bytes 204832 | tf_op jit(solution)/shard_map/ppermute | solution.py:37
  164.2 34.1 %conditional.10 = (bf16[64,1600]{0,1:T(8,128)(2,1)}, bf16[64,1600]{0,1:T(8,128)(2,1)}, f32[1,64,3200]{2,1,0:T(8,128)}, f32[1,64,3200]{2,1,0:T(8,128)}, bf16[1,64...) conditional(s32[]{:T(128)} %convert_element_type.472, ...), branch_computations={%region_5.6_spmd, %region_6.11_spmd} | conditional | flops 3286835456 | bytes 77476808 | solution.py:168
  171.7 5.9 fusion.68
  185.1 9.1 %fusion.36 = bf16[64,1600]{0,1:T(8,128)(2,1)} fusion(bf16[64,3200]{1,0:T(8,128)(2,1)} %get-tuple-element.1010, bf16[3200,1600]{1,0:T(8,128)(2,1)} %get-tuple-element.507, bf16[64,1600]{0,1:T(8,128)(2,1)S(1)} %copy-done.21, f32[128,1600]{0,1:T(8,128)S(1)} %fusion.63), kind=kOutput, calls=%fused_computation.50 | convolution fusion | flops 655769600 | bytes 11468800 | tf_op jit(solution)/shard_map/cond/branch_1_fun/dot_general | solution.py:149
  215.8 35.5 %conditional.11 = (bf16[64,1600]{0,1:T(8,128)(2,1)}, bf16[64,1600]{0,1:T(8,128)(2,1)}, f32[1,64,3200]{2,1,0:T(8,128)}, f32[1,64,3200]{2,1,0:T(8,128)}, bf16[1,64...) conditional(s32[]{:T(128)} %convert_element_type.473, ...), branch_computations={%region_11.12_spmd, %region_12.17_spmd} | conditional | flops 3286835456 | bytes 77476808 | solution.py:168
  225.2 5.9 fusion.107
  238.5 9.1 %fusion.75 = bf16[64,1600]{0,1:T(8,128)(2,1)} fusion(bf16[64,3200]{1,0:T(8,128)(2,1)} %get-tuple-element.1020, bf16[3200,1600]{1,0:T(8,128)(2,1)} %get-tuple-element.514, bf16[64,1600]{0,1:T(8,128)(2,1)S(1)} %copy-done.22, f32[128,1600]{0,1:T(8,128)S(1)} %fusion.102), kind=kOutput, calls=%fused_computation.105 | convolution fusion | flops 655769600 | bytes 11468800 | tf_op jit(solution)/shard_map/cond/branch_1_fun/dot_general | solution.py:149
  277.6 32.4 %collective-permute-start.7 = (bf16[64,1600]{1,0:T(8,128)(2,1)}, bf16[64,1600]{1,0:T(8,128)(2,1)S(1)}, u32[]{:S(2)}, u32[]{:S(2)}) collective-permute-start(bf16[64,1600]{1,0:T(8,128)(2,1)} %copy.197), channel_id=1, source_target_pairs={{0,32},{32,64},{64,96},{1,33},{33,65},{65,97},{2,34},{34,66},{66,9... | collective-permute-start | bytes 614408 | tf_op jit(solution)/shard_map/ppermute | solution.py:37
  352.8 93.9 %collective-permute-done.11 = bf16[64,1600]{1,0:T(8,128)(2,1)S(1)} collective-permute-done((bf16[64,1600]{1,0:T(8,128)(2,1)S(1)}, bf16[64,1600]{1,0:T(8,128)(2,1)S(1)}, u32[]{:S(2)}, u32[]{:S(2)}) %collective-permute-start.11) | collective-permute-done | bytes 204832 | tf_op jit(solution)/shard_map/ppermute | solution.py:37
  451.1 28.6 %conditional.16 = (bf16[64,1600]{0,1:T(8,128)(2,1)}, bf16[64,1600]{0,1:T(8,128)(2,1)}) conditional(s32[]{:T(128)} %convert_element_type.500, () %tuple.165, (bf16[64,1600]{1,0:T(8,128)(2,1)}, f32[2,64,3200]{2,1,0:T(8,128)S(1)}, s32[]{:T(128)}, bf16[64,1600]{1,0:T(8,128)(2,1)S(1)}, bf16[3200,1600]{1,0:T(8,128)(2,1)}, ...), branch_computations={%region_49.50_spmd, %region_50.59_spmd} | conditional | flops 3295233024 | bytes 92612424 | solution.py:238
  453.9 7.6 %fusion.323 = f32[128,3200]{1,0:T(8,128)S(1)} fusion(bf16[3200,1600]{1,0:T(8,128)(2,1)} %get-tuple-element.557, bf16[64,1600]{0,1:T(8,128)(2,1)S(1)} %copy.228, bf16[64,1600]{0,1:T(8,128)(2,1)S(1)} %copy.227), kind=kOutput, calls=%fused_computation.479 | convolution fusion | flops 1311539200 | bytes 12288000 | tf_op jit(solution)/shard_map/cond/branch_1_fun/dot_general | solution.py:73
  461.6 7.4 %fusion.288 = bf16[64,3200]{1,0:T(8,128)(2,1)S(1)} fusion(bf16[64,1600]{1,0:T(8,128)(2,1)S(1)} %copy-done.62, bf16[3200,1600]{1,0:T(8,128)(2,1)} %get-tuple-element.559, f32[128,3200]{1,0:T(8,128)S(1)} %fusion.323, f32[2,64,3200]{2,1,0:T(8,128)S(1)} %copy-done.5, s32[]{:T(128)} %get-tuple-element.555, f32[2,64,3200]{2,1,0:T(8,128)S(1)} %get-tuple-element.554), kind=kOutput, calls=%fused_computation.426 | convolution fusion | flops 661913600 | bytes 14131204 | tf_op jit(solution)/shard_map/cond/branch_1_fun/dot_general | solution.py:73
  494.7 27.1 %conditional.17 = (bf16[64,1600]{0,1:T(8,128)(2,1)}, bf16[64,1600]{0,1:T(8,128)(2,1)}) conditional(s32[]{:T(128)} %convert_element_type.508, () %tuple.167, (bf16[64,1600]{1,0:T(8,128)(2,1)S(1)}, f32[2,64,3200]{2,1,0:T(8,128)S(1)}, s32[]{:T(128)}, bf16[64,1600]{1,0:T(8,128)(2,1)S(1)}, bf16[3200,1600]{1,0:T(8,128)(2,1)}, ...), branch_computations={%region_59.60_spmd, %region_60.69_spmd} | conditional | flops 3295233024 | bytes 87697088 | solution.py:238
  497.2 7.7 %fusion.369 = f32[128,3200]{1,0:T(8,128)S(1)} fusion(bf16[3200,1600]{1,0:T(8,128)(2,1)} %get-tuple-element.568, bf16[64,1600]{0,1:T(8,128)(2,1)S(1)} %copy.234, bf16[64,1600]{0,1:T(8,128)(2,1)} %copy.233), kind=kOutput, calls=%fused_computation.554 | convolution fusion | flops 1311539200 | bytes 12288000 | tf_op jit(solution)/shard_map/cond/branch_1_fun/dot_general | solution.py:73
  504.9 7.4 %fusion.334 = bf16[64,3200]{1,0:T(8,128)(2,1)S(1)} fusion(bf16[64,1600]{1,0:T(8,128)(2,1)S(1)} %get-tuple-element.905, bf16[3200,1600]{1,0:T(8,128)(2,1)} %get-tuple-element.570, f32[128,3200]{1,0:T(8,128)S(1)} %fusion.369, f32[2,64,3200]{2,1,0:T(8,128)S(1)} %copy-done.6, s32[]{:T(128)} %get-tuple-element.566, f32[2,64,3200]{2,1,0:T(8,128)S(1)} %get-tuple-element.565), kind=kOutput, calls=%fused_computation.501 | convolution fusion | flops 661913600 | bytes 14131204 | tf_op jit(solution)/shard_map/cond/branch_1_fun/dot_general | solution.py:73
  545.9 7.4 %all-to-all-start = ((bf16[32,100,128]{2,1,0:T(8,128)(2,1)}), bf16[32,100,128]{2,1,0:T(8,128)(2,1)}, u32[]{:S(2)}, u32[]{:S(2)}) async-start(bf16[32,100,128]{2,1,0:T(8,128)(2,1)} %all_to_all.28), calls=%async_computation | async-start | bytes 1703936 | tf_op jit(solution)/shard_map/all_to_all | solution.py:249
  555.4 20.8 %all-to-all-done = bf16[32,100,128]{2,1,0:T(8,128)(2,1)} async-done(((bf16[32,100,128]{2,1,0:T(8,128)(2,1)}), bf16[32,100,128]{2,1,0:T(8,128)(2,1)}, u32[]{:S(2)}, u32[]{:S(2)}) %all-to-all-start) | async-done | bytes 819232 | tf_op jit(solution)/shard_map/all_to_all | solution.py:249
  576.2 5.6 all-to-all-start.1
  586.9 14.9 %all-to-all-done.1 = bf16[32,100,128]{2,1,0:T(8,128)(2,1)S(1)} async-done(((bf16[32,100,128]{2,1,0:T(8,128)(2,1)}), bf16[32,100,128]{2,1,0:T(8,128)(2,1)S(1)}, u32[]{:S(2)}, u32[]{:S(2)}) %all-to-all-start.1) | async-done | bytes 819232 | tf_op jit(solution)/shard_map/all_to_all | solution.py:248
  602.3 47.9 %all-gather.8.cloned.1.call-done = bf16[4096,3200]{1,0:T(8,128)(2,1)} async-done(((bf16[128,3200]{1,0:T(8,128)(2,1)}), bf16[4096,3200]{1,0:T(8,128)(2,1)}) %all-gather.8.cloned.1.call-update) | async-done | bytes 26214416 | tf_op jit(solution)/shard_map/all_gather | solution.py:46
  650.2 9.1 %fusion.378 = f32[100,1600]{1,0:T(8,128)S(1)} fusion(bf16[100,4096]{1,0:T(8,128)(2,1)S(1)} %bitcast.670, bf16[4096,3200]{1,0:T(8,128)(2,1)} %all-gather.8.cloned.1.call-done), kind=kOutput, calls=%fused_computation.573 | convolution fusion | flops 1310720000 | bytes 15090688 | tf_op jit(solution)/shard_map/dot_general | solution.py:253
  659.4 7.3 fusion.390
  667.4 12.1 %fusion.393 = f32[5,5]{1,0:T(8,128)S(1)} fusion(f32[1,1,100,1600]{3,0,2,1:T(1,128)S(1)} %copy.242, f32[1,1,100,1600]{3,0,2,1:T(1,128)S(1)} %bitcast.667, f32[1,1,100,1600]{3,0,2,1:T(1,128)S(1)} %bitcast.672, f32[2,1,100,1600]{3,0,2,1:T(2,128)S(1)} %copy-done.59), kind=kOutput, calls=%fused_computation.589 | convolution fusion | flops 50400000 | bytes 3200100 | tf_op jit(solution)/shard_map/dot_general | solution.py:258
  679.5 8.8 %psum.28 = f32[5,5]{1,0:T(8,128)S(1)} all-reduce(f32[5,5]{1,0:T(8,128)S(1)} %fusion.393), channel_id=1, replica_groups=mesh['section'=4,'dp_0'=4,'dp_1'=4,'dp_2'=2] {'section'}, use_global_device_ids=true, to_apply=%region_69.70 | all-reduce | flops 25 | bytes 200 | tf_op jit(solution)/shard_map/psum | solution.py:50
  688.2 10.4 %psum.29 = f32[5,5]{1,0:T(8,128)S(1)} all-reduce(f32[5,5]{1,0:T(8,128)S(1)} %psum.28), channel_id=1, replica_groups=mesh['section'=4,'dp_0'=4,'dp_1'=4,'dp_2'=2] {'dp_0'}, use_global_device_ids=true, to_apply=%region_70.71 | all-reduce | flops 25 | bytes 200 | tf_op jit(solution)/shard_map/psum | solution.py:50
  698.7 8.6 %psum.30 = f32[5,5]{1,0:T(8,128)S(1)} all-reduce(f32[5,5]{1,0:T(8,128)S(1)} %psum.29), channel_id=1, replica_groups=mesh['section'=4,'dp_0'=4,'dp_1'=4,'dp_2'=2] {'dp_1'}, use_global_device_ids=true, to_apply=%region_71.72 | all-reduce | flops 25 | bytes 200 | tf_op jit(solution)/shard_map/psum | solution.py:50
  (360 shorter events, 249.0 us)
Async XLA Ops:
  7.2 63.6 %all-gather.4.cloned.1.call-start = ((), (), s32[]{:S(2)}) async-start(), calls=%async_computation.2 | async-start | bytes 5883904 | tf_op jit(solution)/shard_map/all_gather | solution.py:23
  9.1 92.6 %all-gather.6.cloned.1.call-start = ((), (), s32[]{:S(2)}) async-start(), calls=%async_computation.3 | async-start | bytes 15974400 | tf_op jit(solution)/shard_map/all_gather | solution.py:23
  76.4 573.8 %all-gather.8.cloned.1.call-start = ((), (), s32[]{:S(2)}) async-start(), calls=%async_computation.4 | async-start | bytes 27033600 | tf_op jit(solution)/shard_map/all_gather | solution.py:46
  77.7 18.6 %copy-start.32 = (bf16[128,1600]{1,0:T(8,128)(2,1)}, bf16[128,1600]{1,0:T(8,128)(2,1)S(1)}, u32[]{:S(2)}) copy-start(bf16[128,1600]{1,0:T(8,128)(2,1)S(1)} %copy.177) | copy-start | bytes 1228804
  111.7 14.8 %copy-start.64 = (f32[1,1600]{1,0:T(1,128)S(1)}, f32[1,1600]{1,0:T(1,128)}, u32[]{:S(2)}) copy-start(f32[1,1600]{1,0:T(1,128)} %param.32) | copy-start | bytes 19204
  111.7 14.8 %copy-start.67 = (f32[1,3200]{1,0:T(1,128)S(1)}, f32[1,3200]{1,0:T(1,128)}, u32[]{:S(2)}) copy-start(f32[1,3200]{1,0:T(1,128)} %param.31) | copy-start | bytes 38404
  138.4 21.5 %collective-permute-start = (bf16[64,1600]{1,0:T(8,128)(2,1)S(1)}, bf16[64,1600]{1,0:T(8,128)(2,1)S(1)}, u32[]{:S(2)}, u32[]{:S(2)}) collective-permute-start(bf16[64,1600]{1,0:T(8,128)(2,1)S(1)} %get-tuple-element.918), channel_id=1, source_target_pairs={{0,32},{32,64},{64,96},{1,33},{33,65},{65,97},{2,34},{34,66},{66,9... | collective-permute-start | bytes 614408 | tf_op jit(solution)/shard_map/ppermute | solution.py:37
  141.9 22.2 %collective-permute-start.1 = (bf16[64,1600]{1,0:T(8,128)(2,1)S(1)}, bf16[64,1600]{1,0:T(8,128)(2,1)S(1)}, u32[]{:S(2)}, u32[]{:S(2)}) collective-permute-start(bf16[64,1600]{1,0:T(8,128)(2,1)S(1)} %get-tuple-element.919), channel_id=1, source_target_pairs={{0,32},{32,64},{64,96},{1,33},{33,65},{65,97},{2,34},{34,66},{66,9... | collective-permute-start | bytes 614408 | tf_op jit(solution)/shard_map/ppermute | solution.py:37
  145.1 14.8 %copy-start.33 = (bf16[128,1600]{1,0:T(8,128)(2,1)S(1)}, bf16[128,1600]{1,0:T(8,128)(2,1)}, u32[]{:S(2)}) copy-start(bf16[128,1600]{1,0:T(8,128)(2,1)} %copy-done.32) | copy-start | bytes 1228804
  145.2 19.0 %copy-start.2 = (f32[2,64,3200]{2,1,0:T(8,128)}, f32[2,64,3200]{2,1,0:T(8,128)S(1)}, u32[]{:S(2)}) copy-start(f32[2,64,3200]{2,1,0:T(8,128)S(1)} %bitcast_dynamic-update-slice_fusion) | copy-start | bytes 4915204
  201.3 10.3 %collective-permute-start.3 = (bf16[64,1600]{1,0:T(8,128)(2,1)}, bf16[64,1600]{1,0:T(8,128)(2,1)S(1)}, u32[]{:S(2)}, u32[]{:S(2)}) collective-permute-start(bf16[64,1600]{1,0:T(8,128)(2,1)} %copy.189), channel_id=1, source_target_pairs={{0,32},{32,64},{64,96},{1,33},{33,65},{65,97},{2,34},{34,66},{66,9... | collective-permute-start | bytes 614408 | tf_op jit(solution)/shard_map/ppermute | solution.py:37
  203.4 11.6 %collective-permute-start.2 = (bf16[64,1600]{1,0:T(8,128)(2,1)S(1)}, bf16[64,1600]{1,0:T(8,128)(2,1)S(1)}, u32[]{:S(2)}, u32[]{:S(2)}) collective-permute-start(bf16[64,1600]{1,0:T(8,128)(2,1)S(1)} %copy.188), channel_id=1, source_target_pairs={{0,32},{32,64},{64,96},{1,33},{33,65},{65,97},{2,34},{34,66},{66,9... | collective-permute-start | bytes 614408 | tf_op jit(solution)/shard_map/ppermute | solution.py:37
  255.1 10.2 %collective-permute-start.5 = (bf16[64,1600]{1,0:T(8,128)(2,1)}, bf16[64,1600]{1,0:T(8,128)(2,1)S(1)}, u32[]{:S(2)}, u32[]{:S(2)}) collective-permute-start(bf16[64,1600]{1,0:T(8,128)(2,1)} %copy.193), channel_id=1, source_target_pairs={{0,32},{32,64},{64,96},{1,33},{33,65},{65,97},{2,34},{34,66},{66,9... | collective-permute-start | bytes 614408 | tf_op jit(solution)/shard_map/ppermute | solution.py:37
  257.3 10.5 %collective-permute-start.4 = (bf16[64,1600]{1,0:T(8,128)(2,1)}, bf16[64,1600]{1,0:T(8,128)(2,1)S(1)}, u32[]{:S(2)}, u32[]{:S(2)}) collective-permute-start(bf16[64,1600]{1,0:T(8,128)(2,1)} %copy.192), channel_id=1, source_target_pairs={{0,32},{32,64},{64,96},{1,33},{33,65},{65,97},{2,34},{34,66},{66,9... | collective-permute-start | bytes 614408 | tf_op jit(solution)/shard_map/ppermute | solution.py:37
  277.6 38.0 %collective-permute-start.7 = (bf16[64,1600]{1,0:T(8,128)(2,1)}, bf16[64,1600]{1,0:T(8,128)(2,1)S(1)}, u32[]{:S(2)}, u32[]{:S(2)}) collective-permute-start(bf16[64,1600]{1,0:T(8,128)(2,1)} %copy.197), channel_id=1, source_target_pairs={{0,32},{32,64},{64,96},{1,33},{33,65},{65,97},{2,34},{34,66},{66,9... | collective-permute-start | bytes 614408 | tf_op jit(solution)/shard_map/ppermute | solution.py:37
  310.0 7.9 %collective-permute-start.6 = (bf16[64,1600]{1,0:T(8,128)(2,1)}, bf16[64,1600]{1,0:T(8,128)(2,1)S(1)}, u32[]{:S(2)}, u32[]{:S(2)}) collective-permute-start(bf16[64,1600]{1,0:T(8,128)(2,1)} %copy.196), channel_id=1, source_target_pairs={{0,32},{32,64},{64,96},{1,33},{33,65},{65,97},{2,34},{34,66},{66,9... | collective-permute-start | bytes 614408 | tf_op jit(solution)/shard_map/ppermute | solution.py:37
  331.1 9.3 %collective-permute-start.9 = (bf16[64,1600]{1,0:T(8,128)(2,1)S(1)}, bf16[64,1600]{1,0:T(8,128)(2,1)S(1)}, u32[]{:S(2)}, u32[]{:S(2)}) collective-permute-start(bf16[64,1600]{1,0:T(8,128)(2,1)S(1)} %copy.220), channel_id=1, source_target_pairs={{32,0},{64,32},{96,64},{33,1},{65,33},{97,65},{34,2},{66,34},{98,6... | collective-permute-start | bytes 614408 | tf_op jit(solution)/shard_map/ppermute | solution.py:37
  333.0 9.6 %collective-permute-start.8 = (bf16[64,1600]{1,0:T(8,128)(2,1)S(1)}, bf16[64,1600]{1,0:T(8,128)(2,1)S(1)}, u32[]{:S(2)}, u32[]{:S(2)}) collective-permute-start(bf16[64,1600]{1,0:T(8,128)(2,1)S(1)} %copy.219), channel_id=1, source_target_pairs={{32,0},{64,32},{96,64},{33,1},{65,33},{97,65},{34,2},{66,34},{98,6... | collective-permute-start | bytes 614408 | tf_op jit(solution)/shard_map/ppermute | solution.py:37
  347.4 99.4 %collective-permute-start.11 = (bf16[64,1600]{1,0:T(8,128)(2,1)S(1)}, bf16[64,1600]{1,0:T(8,128)(2,1)S(1)}, u32[]{:S(2)}, u32[]{:S(2)}) collective-permute-start(bf16[64,1600]{1,0:T(8,128)(2,1)S(1)} %copy.226), channel_id=1, source_target_pairs={{32,0},{64,32},{96,64},{33,1},{65,33},{97,65},{34,2},{66,34},{98,6... | collective-permute-start | bytes 614408 | tf_op jit(solution)/shard_map/ppermute | solution.py:37
  350.5 98.5 %collective-permute-start.10 = (bf16[64,1600]{1,0:T(8,128)(2,1)S(1)}, bf16[64,1600]{1,0:T(8,128)(2,1)S(1)}, u32[]{:S(2)}, u32[]{:S(2)}) collective-permute-start(bf16[64,1600]{1,0:T(8,128)(2,1)S(1)} %copy.225), channel_id=1, source_target_pairs={{32,0},{64,32},{96,64},{33,1},{65,33},{97,65},{34,2},{66,34},{98,6... | collective-permute-start | bytes 614408 | tf_op jit(solution)/shard_map/ppermute | solution.py:37
  453.9 15.6 %slice-start.6 = ((s8[10240000]{0:T(1024)(128)(4,1)}), s8[4194304]{0:T(1024)(128)(4,1)S(1)}, s32[]{:S(2)}) async-start(s8[10240000]{0:T(1024)(128)(4,1)} %bitcast.621), calls=%async_computation.11 | async-start | bytes 8388608 | tf_op jit(solution)/shard_map/cond
  453.9 15.6 %slice-start.7 = ((s8[10240000]{0:T(1024)(128)(4,1)}), s8[4194304]{0:T(1024)(128)(4,1)S(1)}, s32[]{:S(2)}) async-start(s8[10240000]{0:T(1024)(128)(4,1)} %bitcast.621), calls=%async_computation.12 | async-start | bytes 8388608 | tf_op jit(solution)/shard_map/cond
  480.9 9.6 %collective-permute-start.13 = (bf16[64,1600]{1,0:T(8,128)(2,1)S(1)}, bf16[64,1600]{1,0:T(8,128)(2,1)S(1)}, u32[]{:S(2)}, u32[]{:S(2)}) collective-permute-start(bf16[64,1600]{1,0:T(8,128)(2,1)S(1)} %copy.232), channel_id=1, source_target_pairs={{32,0},{64,32},{96,64},{33,1},{65,33},{97,65},{34,2},{66,34},{98,6... | collective-permute-start | bytes 614408 | tf_op jit(solution)/shard_map/ppermute | solution.py:37
  484.0 8.7 %collective-permute-start.12 = (bf16[64,1600]{1,0:T(8,128)(2,1)S(1)}, bf16[64,1600]{1,0:T(8,128)(2,1)S(1)}, u32[]{:S(2)}, u32[]{:S(2)}) collective-permute-start(bf16[64,1600]{1,0:T(8,128)(2,1)S(1)} %copy.231), channel_id=1, source_target_pairs={{32,0},{64,32},{96,64},{33,1},{65,33},{97,65},{34,2},{66,34},{98,6... | collective-permute-start | bytes 614408 | tf_op jit(solution)/shard_map/ppermute | solution.py:37
  494.7 38.3 %copy-start.1 = (bf16[2,64,1600]{2,1,0:T(8,128)(2,1)S(1)}, bf16[2,64,1600]{2,1,0:T(8,128)(2,1)}, u32[]{:S(2)}) copy-start(bf16[2,64,1600]{2,1,0:T(8,128)(2,1)} %copy-done) | copy-start | bytes 1228804
  497.1 15.7 %slice-start.9 = ((s8[10240000]{0:T(1024)(128)(4,1)}), s8[4194304]{0:T(1024)(128)(4,1)S(1)}, s32[]{:S(2)}) async-start(s8[10240000]{0:T(1024)(128)(4,1)} %bitcast.623), calls=%async_computation.14 | async-start | bytes 8388608 | tf_op jit(solution)/shard_map/cond
  497.2 15.7 %slice-start.10 = ((s8[10240000]{0:T(1024)(128)(4,1)}), s8[4194304]{0:T(1024)(128)(4,1)S(1)}, s32[]{:S(2)}) async-start(s8[10240000]{0:T(1024)(128)(4,1)} %bitcast.623), calls=%async_computation.15 | async-start | bytes 8388608 | tf_op jit(solution)/shard_map/cond
  523.0 10.0 %collective-permute-start.15 = (bf16[64,1600]{1,0:T(8,128)(2,1)S(1)}, bf16[64,1600]{1,0:T(8,128)(2,1)S(1)}, u32[]{:S(2)}, u32[]{:S(2)}) collective-permute-start(bf16[64,1600]{1,0:T(8,128)(2,1)S(1)} %copy.238), channel_id=1, source_target_pairs={{32,0},{64,32},{96,64},{33,1},{65,33},{97,65},{34,2},{66,34},{98,6... | collective-permute-start | bytes 614408 | tf_op jit(solution)/shard_map/ppermute | solution.py:37
  526.5 8.9 %collective-permute-start.14 = (bf16[64,1600]{1,0:T(8,128)(2,1)S(1)}, bf16[64,1600]{1,0:T(8,128)(2,1)S(1)}, u32[]{:S(2)}, u32[]{:S(2)}) collective-permute-start(bf16[64,1600]{1,0:T(8,128)(2,1)S(1)} %copy.237), channel_id=1, source_target_pairs={{32,0},{64,32},{96,64},{33,1},{65,33},{97,65},{34,2},{66,34},{98,6... | collective-permute-start | bytes 614408 | tf_op jit(solution)/shard_map/ppermute | solution.py:37
  545.9 30.3 %all-to-all-start = ((bf16[32,100,128]{2,1,0:T(8,128)(2,1)}), bf16[32,100,128]{2,1,0:T(8,128)(2,1)}, u32[]{:S(2)}, u32[]{:S(2)}) async-start(bf16[32,100,128]{2,1,0:T(8,128)(2,1)} %all_to_all.28), calls=%async_computation | async-start | bytes 1703936 | tf_op jit(solution)/shard_map/all_to_all | solution.py:249
  553.5 29.0 %copy-start.30 = (f32[2,1,100,1600]{3,1,2,0:T(1,128)S(1)}, f32[2,1,100,1600]{3,1,2,0:T(1,128)}, u32[]{:S(2)}) copy-start(f32[2,1,100,1600]{3,1,2,0:T(1,128)} %param.36) | copy-start | bytes 3840004
  576.2 25.5 %all-to-all-start.1 = ((bf16[32,100,128]{2,1,0:T(8,128)(2,1)}), bf16[32,100,128]{2,1,0:T(8,128)(2,1)S(1)}, u32[]{:S(2)}, u32[]{:S(2)}) async-start(bf16[32,100,128]{2,1,0:T(8,128)(2,1)} %all_to_all.32), calls=%async_computation.1 | async-start | bytes 1703936 | tf_op jit(solution)/shard_map/all_to_all | solution.py:248
  (49 other events, 285.8 us)
Sparse Core Ops, SparseCore 0:
  10.7 60.0 all-gather.3
  76.5 25.1 all-gather.5
  539.7 110.4 all-gather.7
where the time goes:
time: 739 us; the launch traced here: 730 us
  waiting for transfers between devices  290 us (39%)
  local copies, waits for them, and re-layouts  118 us (16%)
  matrix products  105 us (14%)
  starting transfers between devices  78.9 us (11%)
  other arithmetic  77.5 us (10%)
  blocking collectives  30.2 us (4%)
  between operations  19 us (3%)
  loops' own time  11.6 us (2%)
    ppermute x16, waiting for transfers between devices, from_behind(): lax.ppermute(value, axis, [(source, source + steps) for source in range(i...  139 us
    all_gather x2, waiting for transfers between devices, gather_in_order(): blocks = lax.all_gather(blocks, axes[k], axis=0, tiled=True)  67 us
    ppermute x16, starting transfers between devices, from_behind(): lax.ppermute(value, axis, [(source, source + steps) for source in range(i...  65.7 us
    all_gather x1, waiting for transfers between devices, sent_together(): lax.all_gather(both, axis, axis=dim, tiled=True)  47.9 us
    select_n x46, other arithmetic, store_block(): jnp.where(active, lax.dynamic_update_index_in_dim(stack, block, position,...  37.7 us
    dot_general x6, matrix products, times_transposed(): lax.dot_general(left, right, (((1,), (1,)), ((), ())), preferred_element_...  36 us
    psum x4, blocking collectives, over_axes(): return functools.reduce(lax.psum, axes, value)  30.2 us
    unnamed x76, local copies, waits for them, and re-layouts  27.3 us
  transfers between devices with their start and end apart: 21, of which 21 were waited for; matrix products, arithmetic and copies ran while one was open for 7% of the time, Pallas kernels for 0%

commit v1 on v0

v1 whole, which is shorter than its diff:
```python
import functools

import jax
import jax.numpy as jnp
from jax import lax
from jax.experimental import pallas as pl
from jax.experimental.pallas import tpu as pltpu
from jax.sharding import PartitionSpec as P

MESH = pl.DeviceIdType.MESH
F32 = jnp.float32
BF16 = jnp.bfloat16

T = 128
D = 1600
FF = 3200
CH = 640
NCH = FF // CH
SH = 100
WIN = 112
CUT = 64
TOKENS = 4096.0
ENTRIES = 20480000.0
GC = 0.7978845608028654
GA = 0.044715


def dot(a, b):
    return jnp.dot(a, b, preferred_element_type=F32)


def dot_t(a, b):
    return lax.dot_general(a, b, (((1,), (1,)), ((), ())), preferred_element_type=F32)


def row_mean(v):
    return jnp.mean(v, axis=1, keepdims=True)


def total(v):
    return jnp.sum(jnp.sum(v, axis=0, keepdims=True), axis=1, keepdims=True)


def mult(v, n):
    return v if isinstance(v, int) else pl.multiple_of(v, n)


def loop(n, fn):
    def step(i, carry):
        fn(i)
        return carry

    lax.fori_loop(0, n, step, 0)


def kernel(
    x_hbm, t_hbm, wi_hbm, bias_hbm, gain_hbm, wo_hbm, cur_hbm, prev_hbm, old_hbm, beta_ref,
    out_ref, tri_ref,
    wi, wo, g, bias, gain, xb, tb, gg, pg, one, two, nb,
    slope, bend, pd, bk, hid, hdot, ht, l0, lp, lr, r1, r2,
    xhat, xdot, acc, mg, ag, rs, rd, pm,
    cur, prev, old, gr, tile, tile2, ar1, ar2,
    lsem, wsem, gsem, hsem, ssem, ysem, yrem, csem, crem, r1sem, r2sem, rss, a1s, a1r, a2s, a2r,
):
    goal = two
    hw = xdot.at[pl.ds(0, WIN)]
    hv = mg.at[pl.ds(0, SH)]
    s = lax.axis_index("section")
    me = lax.axis_index("dp")
    c = lax.rem(me, 2)
    x = me // 8
    z = lax.rem(me // 2, 4)
    p = x * (1 - c) + z * c
    q = z * (1 - c) + x * c

    def m4(v):
        return lax.rem(v + 8, 4)

    def dev_of(pp, qq, cc):
        xx = pp * (1 - cc) + qq * cc
        zz = qq * (1 - cc) + pp * cc
        return (xx * 4 + zz) * 2 + cc

    def dev(pp, qq):
        return dev_of(m4(pp), m4(qq), c)

    partner = me + 1 - 2 * c

    def remote(src, dst, send, recv, sec, dp):
        return pltpu.make_async_remote_copy(
            src_ref=src, dst_ref=dst, send_sem=send, recv_sem=recv,
            device_id=(sec, dp), device_id_type=MESH,
        )

    loads = [
        pltpu.make_async_copy(cur_hbm, cur, lsem.at[0]),
        pltpu.make_async_copy(bias_hbm, bias, lsem.at[1]),
        pltpu.make_async_copy(gain_hbm, gain, lsem.at[2]),
        pltpu.make_async_copy(t_hbm, goal, lsem.at[3]),
        pltpu.make_async_copy(prev_hbm, prev, lsem.at[4]),
        pltpu.make_async_copy(old_hbm, old, lsem.at[5]),
    ]
    x_load = pltpu.make_async_copy(x_hbm, xb, lsem.at[6])
    loads[0].start()

    @pl.when(s == 0)
    def _():
        x_load.start()

    loads[1].start()
    loads[2].start()

    def wi_load(j):
        cols = pl.ds(mult(j * CH, 128), CH)
        return pltpu.make_async_copy(wi_hbm.at[:, cols], wi.at[:, cols], wsem.at[2 * j])

    def wo_load(j):
        cols = pl.ds(mult(j * CH, 128), CH)
        return pltpu.make_async_copy(wo_hbm.at[:, cols], wo.at[:, cols], wsem.at[2 * j + 1])

    for j in range(NCH):
        wi_load(j).start()
        wo_load(j).start()
    for one_load in loads[4:]:
        one_load.start()

    @pl.when(s == 3)
    def _():
        loads[3].start()

    barrier = pltpu.get_barrier_semaphore()

    def greet_section(i, _):
        sec = lax.rem(s + i // 2, 4)
        dp = me + lax.rem(i, 2) * (1 - 2 * c)
        pl.semaphore_signal(barrier, inc=1, device_id=(sec, dp), device_id_type=MESH)
        return _

    def greet_plane(i, _):
        dp = lax.rem(me + 2 * i, 32)
        pl.semaphore_signal(barrier, inc=1, device_id=(s, dp), device_id_type=MESH)
        return _

    lax.fori_loop(1, 8, greet_section, 0)
    lax.fori_loop(1, 16, greet_plane, 0)

    loads[0].wait()
    hw[...] = jnp.zeros((WIN, D), F32)
    for k in range(4):

        @pl.when(lax.rem(me, 4) == k)
        def _(k=k):
            hw[4 * k:4 * k + SH, :] = cur[...]

    def win(d):
        return g.at[pl.ds(mult(d * WIN, 16), WIN)]

    def win_part(d, half):
        if half == 0:
            return g.at[pl.ds(mult(d * WIN, 16), CUT)]
        return g.at[pl.ds(mult(d * WIN + CUT, 16), WIN - CUT)]

    g[pl.ds(mult(me * WIN, 16), WIN), :] = hw[...].astype(BF16)
    pl.semaphore_wait(barrier, 22)

    a_up, a_down, b_up, b_down = dev(p + 1, q), dev(p - 1, q), dev(p, q + 1), dev(p, q - 1)
    far = dev(p + 2, q)
    w_b = [dev(p, q - 1), dev(p - 1, q - 1), dev(p + 1, q - 1), dev(p + 2, q - 1)]
    w_u = [dev(p, q + 1), dev(p - 1, q + 1), dev(p + 1, q + 1), dev(p + 2, q + 1)]
    w_f = [dev(p, q + 2), dev(p - 1, q + 2), dev(p + 1, q + 2), dev(p + 2, q + 2)]

    first_steps = [
        ([(a_down, None)], [(a_down, 0, a_up), (a_down, None, b_up), (a_down, None, b_down), (a_down, None, partner)]),
        ([(a_up, None)], [(a_up, 1, a_down), (a_up, None, b_up), (a_up, None, b_down), (a_up, None, partner)]),
        ([(w_b[0], None)], [(w_b[0], None, b_up), (w_b[0], None, partner)]),
        ([(w_u[0], None)], [(w_u[0], None, partner)]),
        ([(far, 0), (far, 1)], [(far, None, b_up), (far, None, b_down), (far, None, partner)]),
    ]
    rest_steps = [
        ([(w_b[1], None)], [(w_b[1], None, b_up), (w_b[1], None, partner)]),
        ([(w_u[2], None)], [(w_u[2], None, b_down), (w_u[2], None, partner)]),
        ([(w_u[1], None)], [(w_u[1], None, partner)]),
        ([(w_b[2], None)], [(w_b[2], None, partner)]),
        ([(w_u[3], None)], [(w_u[3], None, b_down), (w_u[3], None, partner)]),
    ]
    rest_steps += [([(d, None)], [(d, None, partner)]) for d in [w_b[3]] + w_f]
    own_sends = [(me, None, to) for to in (a_up, a_down, b_up, b_down, partner)]
    plan = own_sends + [send for _, sent in first_steps + rest_steps for send in sent]

    def share(i):
        d, part, to = plan[i]
        if part is None:
            return remote(win(d), win(d), ssem.at[i], gsem.at[d], s, to)
        return remote(win_part(d, part), win_part(d, part), ssem.at[i], hsem.at[part], s, to)

    def got(d, part=None):
        if part is None:
            remote(win(d), win(d), ssem.at[0], gsem.at[d], s, partner).wait_recv()
        else:
            ref = win_part(d, part)
            remote(ref, ref, ssem.at[0], hsem.at[part], s, partner).wait_recv()

    def run_steps(steps, at):
        for waits, sent in steps:
            for d, part in waits:
                got(d, part)
            for _ in sent:
                share(at).start()
                at += 1
        return at

    rest_at = len(own_sends) + sum(len(sent) for _, sent in first_steps)
    for i in range(len(own_sends)):
        share(i).start()

    def gather_first():
        run_steps(first_steps, len(own_sends))

    def gather_rest():
        run_steps(rest_steps, rest_at)

        def other(k):
            got(2 * k + 1 - c)

        loop(16, other)
        for i in range(len(plan)):
            share(i).wait_send()

        def pack(i):
            src = mult(i * (4 * WIN), 16)
            dst = mult(i * (4 * SH), 16)
            for k in range(4):
                value = g[pl.ds(src + k * WIN, WIN), :]
                at = dst + k * 96
                if k == 0:
                    g[pl.ds(at, WIN), :] = value
                else:
                    edge = g[pl.ds(at, 16), :].astype(F32) + value[:16].astype(F32)
                    g[pl.ds(at, 16), :] = edge.astype(BF16)
                    g[pl.ds(at + 16, WIN - 16), :] = value[16:]

        loop(8, pack)

    def hop(k):
        src = (one, two, one, two)[k]
        dst = (xb, tb, gg.at[pl.ds(0, T)], gg.at[pl.ds(T, T)])[k]
        to = lax.rem(s + (1 if k < 2 else 3), 4)
        return remote(src, dst, ysem.at[k], yrem.at[k], to, me)

    def cols(j):
        return pl.ds(mult(j * CH, 128), CH)

    def rows(j):
        return pl.ds(mult(j * CH, 16), CH)

    def forward():
        @pl.when(s == 0)
        def _():
            x_load.wait()

        loads[1].wait()
        loads[2].wait()

        @pl.when(s > 0)
        def _():
            hop(0).wait_recv()

        rows_in = xb[...].astype(F32)
        centered = rows_in - row_mean(rows_in)
        r = lax.rsqrt(row_mean(centered * centered) + 1e-05)
        hat = centered * r
        rs[...] = r
        xhat[...] = hat
        nb[...] = (hat * gain[...]).astype(BF16)
        acc[...] = jnp.zeros((T, D), F32)

        def chunk(j):
            wi_load(j).wait()
            wo_load(j).wait()
            v = dot(nb[...], wi[:, cols(j)]) + bias[:, cols(j)]
            v2 = v * v
            t = jnp.tanh(GC * (v + GA * (v * v2)))
            h = (0.5 * v * (1.0 + t)).astype(BF16)
            hid[:, cols(j)] = h
            acc[...] += dot_t(h, wo[:, cols(j)])
            up = GC * (1.0 + (3.0 * GA) * v2)
            om = 1.0 - t * t
            slope[:, cols(j)] = 0.5 * (1.0 + t) + 0.5 * v * om * up
            bend[:, cols(j)] = om * (up + 0.5 * v * ((6.0 * GC * GA) * v - 2.0 * t * up * up))

        loop(NCH, chunk)
        one[...] = (xb[...].astype(F32) + acc[...]).astype(BF16)

        @pl.when(s < 3)
        def _():
            hop(0).start()

        @pl.when(s == 3)
        def _():
            loads[3].wait()
            gg[0:T, :] = ((one[...].astype(F32) - goal[...].astype(F32)) * (1.0 / TOKENS)).astype(BF16)

    def gather_and_forward(k):
        @pl.when(k == 1)
        def _():
            gather_first()

        @pl.when(k == 2)
        def _():
            gather_rest()

        @pl.when(k == jnp.minimum(s, 2))
        def _():
            forward()

    loop(3, gather_and_forward)

    @pl.when(s < 3)
    def _():
        hop(0).wait_send()

    def swap(k):
        src = (lp, gg.at[pl.ds(0, T)], gg.at[pl.ds(T, T)])[k]
        dst = (lr, pg.at[pl.ds(0, T)], pg.at[pl.ds(T, T)])[k]
        return remote(src, dst, csem.at[k], crem.at[k], s, partner)

    def tangent():
        acc[...] = jnp.zeros((T, D), F32)

        def early(j):
            acc[...] += dot(hid[:, cols(j)], g[rows(j), :])

        loop(NCH, early)

        @pl.when(s > 0)
        def _():
            hop(1).wait_recv()
            tan = tb[...].astype(F32)
            moved = tan - row_mean(tan)
            hat = xhat[...]
            r = rs[...]
            along = row_mean(hat * moved)
            hat_dot = r * (moved - hat * along)
            rd[...] = -(r * r) * along
            xdot[...] = hat_dot
            nb[...] = (hat_dot * gain[...]).astype(BF16)

            def chunk(j):
                v = dot(nb[...], wi[:, cols(j)])
                pd[:, cols(j)] = v
                h = (slope[:, cols(j)] * v).astype(BF16)
                hdot[:, cols(j)] = h
                acc[...] += dot_t(h, wo[:, cols(j)])

            loop(NCH, chunk)
            two[...] = (tb[...].astype(F32) + acc[...]).astype(BF16)

        @pl.when(s == 0)
        def _():
            two[...] = acc[...].astype(BF16)

        @pl.when(s < 3)
        def _():
            hop(1).start()

        @pl.when(s == 3)
        def _():
            gg[T:2 * T, :] = (two[...].astype(F32) * (1.0 / TOKENS)).astype(BF16)

        @pl.when(s == 0)
        def _():
            ht[:, 0:T] = jnp.zeros((FF, T), BF16)

        def turn(j):
            ht[rows(j), T:2 * T] = hid[:, cols(j)].astype(F32).T.astype(BF16)

            @pl.when(s > 0)
            def _():
                ht[rows(j), 0:T] = hdot[:, cols(j)].astype(F32).T.astype(BF16)

        loop(NCH, turn)

        def line_up(i):
            e, a = i // 4, lax.rem(i, 4)
            to = pl.ds(mult(i * WIN, 16), WIN)
            shift = (e == 0) * 2 + (e == 1) * 1 + (e == 2) * 3
            mine = dev_of(a, m4(q + shift), c)
            theirs = dev_of(a, m4(p + shift), 1 - c)
            l0[to, :] = ht[pl.ds(mult(mine * SH - 4 * lax.rem(mine, 4), 16), WIN), :]
            lp[to, :] = ht[pl.ds(mult(theirs * SH - 4 * lax.rem(theirs, 4), 16), WIN), :]

        loop(16, line_up)
        swap(0).start()

    def backward():
        @pl.when(s < 3)
        def _():
            hop(2).wait_recv()

        swap(1).start()

        @pl.when(s > 0)
        def _():
            acc[...] = jnp.zeros((T, D), F32)

            def chunk(j):
                v = dot(gg[0:T, :], wo[:, cols(j)])
                bk[:, cols(j)] = v
                pre = (slope[:, cols(j)] * v).astype(BF16)
                acc[...] += dot_t(pre, wi[:, cols(j)])

            loop(NCH, chunk)
            m = acc[...] * gain[...]
            hat = xhat[...]
            p_mean = row_mean(m * hat)
            a = m - row_mean(m) - hat * p_mean
            mg[...] = m
            ag[...] = a
            pm[...] = p_mean
            one[...] = (gg[0:T, :].astype(F32) + rs[...] * a).astype(BF16)
            hop(2).start()

    def tangent_and_backward(k):
        @pl.when(k == 1)
        def _():
            tangent()

        @pl.when(k == jnp.where(s == 3, 0, 2))
        def _():
            backward()

    loop(3, tangent_and_backward)

    @pl.when(s < 3)
    def _():
        hop(1).wait_send()

    @pl.when(s > 0)
    def _():
        def chunk(j):
            v = dot_t(gg[0:T, :], g[rows(j), :])
            bk[:, cols(j)] = bend[:, cols(j)] * pd[:, cols(j)] * bk[:, cols(j)] + slope[:, cols(j)] * v

        loop(NCH, chunk)

    lane = lax.broadcasted_iota(jnp.int32, (8, 128), 1)
    loads[4].wait()
    loads[5].wait()

    def member(i):
        return (old[0], old[1], prev[...], cur[...])[i]

    grams = jnp.zeros((8, 128), F32)
    for i in range(4):
        for j in range(i, 4):
            grams = jnp.where(lane == 5 * i + j, total(member(i) * member(j)), grams)
    gr[...] = grams

    @pl.when(s < 3)
    def _():
        hop(3).wait_recv()

    swap(2).start()

    @pl.when(s > 0)
    def _():
        acc[...] = jnp.zeros((T, D), F32)

        def chunk(j):
            v = dot(gg[T:2 * T, :], wo[:, cols(j)])
            pre = (bk[:, cols(j)] + slope[:, cols(j)] * v).astype(BF16)
            acc[...] += dot_t(pre, wi[:, cols(j)])

        loop(NCH, chunk)
        m_dot = acc[...] * gain[...]
        hat = xhat[...]
        hat_dot = xdot[...]
        p_dot = row_mean(m_dot * hat) + row_mean(mg[...] * hat_dot)
        a_dot = m_dot - row_mean(m_dot) - hat_dot * pm[...] - hat * p_dot
        moved = rd[...] * ag[...] + rs[...] * a_dot
        two[...] = (gg[T:2 * T, :].astype(F32) + moved).astype(BF16)
        hop(3).start()

    for k in range(3):
        swap(k).wait_recv()

    def slots(i, n):
        return pl.ds(i * WIN, n * WIN)

    def rs_copy(k):
        src = g.at[(slots(0, 2), slots(2, 2), slots(6, 2), slots(4, 2), slots(8, 2), slots(10, 2))[k]]
        dst = r1.at[(slots(0, 2), slots(6, 2), slots(4, 2), slots(2, 2), slots(8, 2), slots(10, 2))[k]]
        to = (b_up, b_down, b_up, b_up, b_down, b_down)[k]
        return remote(src, dst, rss.at[k], r1sem.at[k], s, to)

    def piece(e):
        at = pl.ds(mult(e * (4 * WIN), 16), 4 * WIN)
        left = jnp.concatenate([l0[at, :], lr[at, :]], axis=1)
        for lo, hi in ((0, 512), (512, 1024), (1024, D)):
            right = jnp.concatenate([gg[:, lo:hi], pg[:, lo:hi]], axis=0)
            g[at, lo:hi] = dot(left, right).astype(BF16)

        @pl.when(e == 0)
        def _():
            rs_copy(0).start()
            rs_copy(1).start()

        @pl.when(e == 1)
        def _():
            rs_copy(2).start()

        @pl.when(e == 2)
        def _():
            rs_copy(4).start()

    loop(4, piece)

    def add_into(at, other, n):
        g[at, :] = (g[at, :].astype(F32) + other[...].astype(F32)).astype(BF16)

    rs_copy(0).wait_recv()
    add_into(slots(4, 2), r1.at[slots(0, 2)], 2)
    rs_copy(3).start()
    rs_copy(1).wait_recv()
    add_into(slots(10, 2), r1.at[slots(6, 2)], 2)
    rs_copy(5).start()
    for k in (2, 4, 3, 5):
        rs_copy(k).wait_recv()

    def own_slot(a):
        return mult((12 + a) * WIN, 16)

    def summed(a):
        v = g[pl.ds(own_slot(a), WIN), :].astype(F32)
        v += r1[pl.ds(mult((2 + a) * WIN, 16), WIN), :].astype(F32)
        v += r1[pl.ds(mult((8 + a) * WIN, 16), WIN), :].astype(F32)
        return v

    tail = WIN - CUT

    def part(a, half):
        if half == 0:
            return pl.ds(own_slot(a), CUT)
        return pl.ds(mult(own_slot(a) + CUT, 16), tail)

    a_far, a_next, a_last = m4(p + 2), m4(p + 1), m4(p - 1)

    def rs2_copy(k):
        src = (part(a_far, 0), part(a_far, 1), part(a_next, 1), part(a_next, 0), part(a_last, 0), part(a_last, 1))[k]
        dst = (
            pl.ds(0, CUT), pl.ds(CUT, tail), pl.ds(WIN + CUT, tail), pl.ds(WIN, CUT),
            pl.ds(2 * WIN, CUT), pl.ds(2 * WIN + CUT, tail),
        )[k]
        to = (a_up, a_down, a_up, a_up, a_down, a_down)[k]
        return remote(g.at[src], r2.at[dst], rss.at[6 + k], r2sem.at[k], s, to)

    g[pl.ds(own_slot(a_far), WIN), :] = summed(a_far).astype(BF16)
    rs2_copy(0).start()
    rs2_copy(1).start()
    g[pl.ds(own_slot(a_next), WIN), :] = summed(a_next).astype(BF16)
    rs2_copy(2).start()
    g[pl.ds(own_slot(a_last), WIN), :] = summed(a_last).astype(BF16)
    rs2_copy(4).start()
    hw[...] = summed(p)
    rs2_copy(0).wait_recv()
    add_into(part(a_next, 0), r2.at[pl.ds(0, CUT)], 1)
    rs2_copy(3).start()
    rs2_copy(1).wait_recv()
    add_into(part(a_last, 1), r2.at[pl.ds(CUT, tail)], 1)
    rs2_copy(5).start()
    for k in (2, 4, 3, 5):
        rs2_copy(k).wait_recv()
    hw[...] += r2[WIN:2 * WIN, :].astype(F32) + r2[2 * WIN:3 * WIN, :].astype(F32)
    for k in range(4):

        @pl.when(lax.rem(me, 4) == k)
        def _(k=k):
            hv[...] = hw[4 * k:4 * k + SH, :]

    grams = gr[...]
    for i in range(4):
        grams = jnp.where(lane == 5 * i + 4, total(member(i) * hv[...]), grams)
    grams = jnp.where(lane == 24, total(hv[...] * hv[...]), grams)
    tile[...] = grams

    mine1 = s * 2 + c

    def a1_copy(i):
        sec = lax.rem(s + i // 2, 4)
        dp = me + lax.rem(i, 2) * (1 - 2 * c)
        return remote(tile, ar1.at[mine1], a1s.at[i], a1r.at[mine1], sec, dp)

    def a1_wait(i):
        them = lax.rem(s + i // 2, 4) * 2 + lax.rem(c + i, 2)
        remote(tile, ar1.at[them], a1s.at[i], a1r.at[them], s, partner).wait_recv()

    def span(lo, hi, fn):
        def step(i, carry):
            fn(i)
            return carry

        lax.fori_loop(lo, hi, step, 0)

    span(1, 8, lambda i: a1_copy(i).start())
    ar1[mine1] = grams
    span(1, 8, a1_wait)
    level = ar1[0]
    for i in range(1, 8):
        level = level + ar1[i]
    tile2[...] = level
    mine2 = me // 2

    def a2_copy(i):
        dp = lax.rem(me + 2 * i, 32)
        return remote(tile2, ar2.at[mine2], a2s.at[i], a2r.at[mine2], s, dp)

    def a2_wait(i):
        them = lax.rem(mine2 + i, 16)
        remote(tile2, ar2.at[them], a2s.at[i], a2r.at[them], s, partner).wait_recv()

    span(1, 16, lambda i: a2_copy(i).start())
    ar2[mine2] = level
    span(1, 16, a2_wait)
    level = ar2[0]
    for i in range(1, 16):
        level = level + ar2[i]
    level = level[0:1, :] * (1.0 / ENTRIES)
    lane1 = lane[0:1, :]

    def entry(i, j):
        i, j = min(i, j), max(i, j)
        return jnp.sum(jnp.where(lane1 == 5 * i + j, level, 0.0), axis=1, keepdims=True)

    gram = [[entry(i, j) for j in range(5)] for i in range(4)]
    square = entry(4, 4)
    start = jnp.full((1, 1), -beta_ref[0], F32)
    alpha = gram[3][4] + start * gram[2][3]
    first = [None, None, start, -alpha]
    weights = []
    for j in range(4):
        coeff = gram[j][4] + start * gram[2][j] - alpha * gram[3][j]
        weights.append(-coeff if first[j] is None else first[j] - coeff)
    norm = square
    for i in range(4):
        norm = norm + 2.0 * weights[i] * gram[i][4]
        for j in range(4):
            norm = norm + weights[i] * gram[i][j] * weights[j]
    beta = jnp.sqrt(jnp.maximum(norm, 0.0) + 1e-06)
    second = hv[...]
    for j in range(4):
        second = second + weights[j] * member(j)
    out_ref[...] = second / beta
    tri_ref[...] = jnp.where(lane == 0, alpha, jnp.where(lane == 1, beta, 0.0))

    for k in range(3):
        swap(k).wait_send()

    @pl.when(s > 0)
    def _():
        hop(2).wait_send()
        hop(3).wait_send()

    for k in range(6):
        rs_copy(k).wait_send()
        rs2_copy(k).wait_send()
    span(1, 8, lambda i: a1_copy(i).wait_send())
    span(1, 16, lambda i: a2_copy(i).wait_send())


def body(inputs, targets, weight_in, hidden_bias, norm_gain, weight_out, current, previous, older_basis, beta_before):
    any_spec = pl.BlockSpec(memory_space=pl.ANY)
    vmem = pltpu.VMEM
    dma = pltpu.SemaphoreType.DMA
    scratch = [
        vmem((D, FF), BF16),
        vmem((D, FF), BF16),
        vmem((32 * WIN, D), BF16),
        vmem((1, FF), F32),
        vmem((1, D), F32),
        vmem((T, D), BF16),
        vmem((T, D), BF16),
        vmem((2 * T, D), BF16),
        vmem((2 * T, D), BF16),
        vmem((T, D), BF16),
        vmem((T, D), BF16),
        vmem((T, D), BF16),
        vmem((T, FF), F32),
        vmem((T, FF), F32),
        vmem((T, FF), F32),
        vmem((T, FF), F32),
        vmem((T, FF), BF16),
        vmem((T, FF), BF16),
        vmem((FF, 2 * T), BF16),
        vmem((16 * WIN, 2 * T), BF16),
        vmem((16 * WIN, 2 * T), BF16),
        vmem((16 * WIN, 2 * T), BF16),
        vmem((12 * WIN, D), BF16),
        vmem((3 * WIN, D), BF16),
        vmem((T, D), F32),
        vmem((T, D), F32),
        vmem((T, D), F32),
        vmem((T, D), F32),
        vmem((T, D), F32),
        vmem((T, 1), F32),
        vmem((T, 1), F32),
        vmem((T, 1), F32),
        vmem((SH, D), F32),
        vmem((SH, D), F32),
        vmem((2, SH, D), F32),
        vmem((8, 128), F32),
        vmem((8, 128), F32),
        vmem((8, 128), F32),
        vmem((8, 8, 128), F32),
        vmem((16, 8, 128), F32),
        dma((7,)),
        dma((2 * NCH,)),
        dma((32,)),
        dma((2,)),
        dma((34,)),
        dma((4,)),
        dma((4,)),
        dma((3,)),
        dma((3,)),
        dma((6,)),
        dma((6,)),
        dma((12,)),
        dma((8,)),
        dma((8,)),
        dma((16,)),
        dma((16,)),
    ]
    out, tri = pl.pallas_call(
        kernel,
        out_shape=(
            jax.ShapeDtypeStruct((SH, D), F32),
            jax.ShapeDtypeStruct((8, 128), F32),
        ),
        in_specs=[any_spec] * 9 + [pl.BlockSpec(memory_space=pltpu.SMEM)],
        out_specs=(pl.BlockSpec(memory_space=pltpu.VMEM), pl.BlockSpec(memory_space=pltpu.VMEM)),
        scratch_shapes=scratch,
        compiler_params=pltpu.CompilerParams(
            collective_id=0, has_side_effects=True, vmem_limit_bytes=67043328
        ),
    )(
        inputs, targets, weight_in[0], hidden_bias, norm_gain, weight_out[0].T,
        current[0], previous[0], older_basis[:, 0], beta_before,
    )
    return out[None], tri[0, :2]


def solution(mesh):
    dp = "dp"
    in_specs = (
        P(dp, None),
        P(dp, None),
        P("section", None, None),
        P("section", None),
        P("section", None),
        P("section", None, None),
        P("section", dp, None),
        P("section", dp, None),
        P(None, "section", dp, None),
        P(),
    )
    out_specs = (P("section", dp, None), P())
    return jax.shard_map(body, mesh=mesh, in_specs=in_specs, out_specs=out_specs, check_vma=False)
```

time: 739 us -> 214 us (0.29); the launches traced: 730 us -> 214 us
  waiting for transfers between devices: 290 us -> 0 us
  Pallas kernels: 0 us -> 200 us
  local copies, waits for them, and re-layouts: 118 us -> 12.7 us
  matrix products: 105 us -> 0 us
  starting transfers between devices: 78.9 us -> 0 us
  other arithmetic: 77.5 us -> 0 us
  blocking collectives: 30.2 us -> 0 us
  between operations: 19 us -> 1.29 us
  loops' own time: 11.6 us -> 0 us
    pallas_call x0 -> x1, Pallas kernels: none -> 200 us  [body(): pl.pallas_call(kernel, out_shape=(jax.ShapeDtypeStruct((SH, D), F32), jax...]
    ppermute x16 -> x0, waiting for transfers between devices: 139 us -> none  [from_behind(): lax.ppermute(value, axis, [(source, source + steps) for source in range(i...]
    all_gather x3 -> x0, waiting for transfers between devices: 115 us -> none  [the longest x2 67 us: gather_in_order(): blocks = lax.all_gather(blocks, axes[k], axis=0, tiled=True)]
    dot_general x15 -> x0, matrix products: 105 us -> none  [the longest x6 36 us: times_transposed(): lax.dot_general(left, right, (((1,), (1,)), ((), ())), preferred_element_...]
    ppermute x16 -> x0, starting transfers between devices: 65.7 us -> none  [from_behind(): lax.ppermute(value, axis, [(source, source + steps) for source in range(i...]
    select_n x46 -> x0, other arithmetic: 37.7 us -> none  [store_block(): jnp.where(active, lax.dynamic_update_index_in_dim(stack, block, position,...]
    all_to_all x2 -> x0, waiting for transfers between devices: 35.7 us -> none  [the longest x1 20.8 us: body(): lax.all_to_all(hidden_dot_rows.T, DP, split_axis=0, concat_axis=1, tiled=...]
    psum x4 -> x0, blocking collectives: 30.2 us -> none  [over_axes(): return functools.reduce(lax.psum, axes, value)]
  transfers between devices with their start and end apart: 21 -> 0, of which waited for: 21 -> 0; matrix products, arithmetic and copies ran while one was open for 7% -> 0% of each run, Pallas kernels for 0% -> 0%
where the time goes in v1:
time: 214 us
  Pallas kernels  200 us (93%)
  local copies, waits for them, and re-layouts  12.7 us (6%)
    pallas_call x1, Pallas kernels, body(): pl.pallas_call(kernel, out_shape=(jax.ShapeDtypeStruct((SH, D), F32), jax...  200 us
    unnamed x5, local copies, waits for them, and re-layouts  11.5 us

profile of v1, /device:TPU:8, one launch (start us, length us, event | category | flops | bytes accessed | tf_op | source)
XLA Modules:
  0.0 213.9 jit_solution(14445977371156574683)
XLA Ops:
  1.3 2.0 copy.15.x_hbm
  3.2 2.0 copy.16.t_hbm
  5.2 2.5 %copy.24 = f32[2,1,100,1600]{3,2,1,0:T(8,128)} copy(f32[2,1,100,1600]{3,1,2,0:T(1,128)} %param.18) | data formatting | bytes 2560000
  7.7 2.5 %copy_bitcast_fusion.1 = (f32[100,1600]{1,0:T(8,128)}, f32[100,1600]{1,0:T(8,128)}) fusion(f32[1,100,1600]{2,0,1:T(1,128)} %param.17, f32[1,100,1600]{2,0,1:T(1,128)} %param.16), kind=kLoop, calls=%fused_computation.1 | loop fusion | bytes 2560000
  10.2 199.9 %shard_map.113 = (f32[100,1600]{1,0:T(8,128)}, f32[8,128]{1,0:T(8,128)}) custom-call(bf16[128,1600]{1,0:T(8,128)(2,1)} %copy.15.x_hbm, bf16[128,1600]{1,0:T(8,128)(2,1)} %copy.16.t_hbm, bf16[1600,3200]{1,0:T(8,128)(2,1)} %bitcast.14, f32[1,3200]{1,0:T(1,128)} %bias_hbm.1, f32[1,1600]{1,0:T(1,128)} %gain_hbm.1, bf16[1600,3200]{1,0:T(8,128)(2,1)} %bitcast.15, ...), custom_call_target="tpu_custom_call" | custom-call | tf_op jit(solution)/shard_map/pallas_call | solution.py:732
  210.1 2.6 %copy.17 = f32[1,100,1600]{2,0,1:T(1,128)} copy(f32[1,100,1600]{2,1,0:T(8,128)} %bitcast.17) | data formatting | bytes 1280000
  212.7 1.2 slice_bitcast_fusion
